TPU v7x, 32 devices: a whole 2x2x4 slice. The times are simulated.
32 devices in a mesh: fsdp: 8 (over y, x, core), rep: 4 (over z).
Axes of the slice: x: 2, y: 2, z: 4, core: 2. Of those that a mesh axis runs over, the one named last changes fastest.
Arguments:
- hidden_in: bfloat16 [64, 512, 768], P(('fsdp', 'rep')), may hold values from -6 to 6
- lengths: int32 [64], P(('fsdp', 'rep')), may hold values from 128 to 512, as said below
- query_weight: bfloat16 [768, 768], P(('fsdp', 'rep')), may hold values from -0.21875 to 0.21875
- key_weight: bfloat16 [768, 768], P(('fsdp', 'rep')), may hold values from -0.21875 to 0.21875
- value_weight: bfloat16 [768, 768], P(('fsdp', 'rep')), may hold values from -0.21875 to 0.21875
- out_weight: bfloat16 [768, 768], P(('fsdp', 'rep')), may hold values from -3 to 3
- up_weight: bfloat16 [768, 3072], P(('fsdp', 'rep')), may hold values from -0.21875 to 0.21875
- down_weight: bfloat16 [3072, 768], P(('fsdp', 'rep')), may hold values from -0.109375 to 0.109375
- query_bias: bfloat16 [768], P(('fsdp', 'rep')), may hold values from -1.796875 to 1.796875
- value_bias: bfloat16 [768], P(('fsdp', 'rep')), may hold values from -1.796875 to 1.796875
- out_bias: bfloat16 [768], P(('fsdp', 'rep')), may hold values from -1.796875 to 1.796875
- up_bias: bfloat16 [3072], P(('fsdp', 'rep')), may hold values from -1.796875 to 1.796875
- down_bias: bfloat16 [768], P(('fsdp', 'rep')), may hold values from -1.796875 to 1.796875
- first_gain: bfloat16 [768], P(('fsdp', 'rep')), may hold values from 0.5 to 1.5
- first_shift: bfloat16 [768], P(('fsdp', 'rep')), may hold values from -1.796875 to 1.796875
- second_gain: bfloat16 [768], P(('fsdp', 'rep')), may hold values from 0.5 to 1.5
- second_shift: bfloat16 [768], P(('fsdp', 'rep')), may hold values from -1.796875 to 1.796875
- cotangent: bfloat16 [64, 512, 768], P(('fsdp', 'rep')), may hold values from -6 to 6
Outputs:
- hidden_out: bfloat16 [64, 512, 768], P(('fsdp', 'rep'))
- input_grad: bfloat16 [64, 512, 768], P(('fsdp', 'rep'))
- query_weight_grad: float32 [768, 768], P(('fsdp', 'rep'))
- key_weight_grad: float32 [768, 768], P(('fsdp', 'rep'))
- value_weight_grad: float32 [768, 768], P(('fsdp', 'rep'))
- out_weight_grad: float32 [768, 768], P(('fsdp', 'rep'))
- up_weight_grad: float32 [768, 3072], P(('fsdp', 'rep'))
- down_weight_grad: float32 [3072, 768], P(('fsdp', 'rep'))
- query_bias_grad: float32 [768], P(('fsdp', 'rep'))
- value_bias_grad: float32 [768], P(('fsdp', 'rep'))
- out_bias_grad: float32 [768], P(('fsdp', 'rep'))
- up_bias_grad: float32 [3072], P(('fsdp', 'rep'))
- down_bias_grad: float32 [768], P(('fsdp', 'rep'))
- first_gain_grad: float32 [768], P(('fsdp', 'rep'))
- first_shift_grad: float32 [768], P(('fsdp', 'rep'))
- second_gain_grad: float32 [768], P(('fsdp', 'rep'))
- second_shift_grad: float32 [768], P(('fsdp', 'rep'))
Inputs may be any that keep to these rules, and one draw needn't show every extreme that they name: `lengths`: one sequence fills all 512 slots and one has the fewest valid tokens.
All inputs are finite; a program needn't handle non-finite values.
Results may differ from a plain program's by a relative error of at most 0.015.
Values may be sent and summed in bfloat16 or wider, within the bound.
A program may use at most 192 MiB of HBM per device.

v0:
```python
import functools
import math

import jax
import jax.numpy as jnp
from jax import lax
from jax.experimental import pallas as pl
from jax.experimental.pallas import tpu as pltpu
from jax.sharding import PartitionSpec as P

HD = 64
PAIR = 2 * HD
BF = jnp.bfloat16
F32 = jnp.float32


def nt(left, right):
    return lax.dot_general(left, right, (((1,), (1,)), ((), ())), preferred_element_type=F32)


def nn(left, right):
    return jnp.dot(left, right, preferred_element_type=F32)


def tn(left, right):
    return lax.dot_general(left, right, (((0,), (0,)), ((), ())), preferred_element_type=F32)


def head_masks(length):
    lane = lax.broadcasted_iota(jnp.int32, (length, PAIR), 1)
    return lane


def masked_keys(k2, lane, head, valid):
    inside = (lane // HD) == head
    slot = lane == (1 - head) * HD
    row = lax.broadcasted_iota(jnp.int32, lane.shape, 0)
    bias = jnp.where(row < valid, 0.0, -1e30).astype(BF)
    return jnp.where(inside, k2, jnp.where(slot, bias, jnp.zeros_like(k2)))


def masked_query(q2, lane, head):
    inside = (lane // HD) == head
    slot = lane == (1 - head) * HD
    return jnp.where(inside, q2, jnp.where(slot, jnp.ones_like(q2), jnp.zeros_like(q2)))


def forward_pair(valid, q2, k2, v2):
    lane = head_masks(q2.shape[0])
    first = lane < HD
    q2 = q2 * BF(0.125)
    outs, tops = [], []
    for h in (0, 1):
        s = nt(masked_query(q2, lane, h), masked_keys(k2, lane, h, valid))
        top = jnp.max(s, axis=1, keepdims=True)
        e = jnp.exp(s - top).astype(BF)
        outs.append(nn(e, jnp.where((lane // HD) == h, v2, jnp.ones_like(v2))))
        tops.append(top)
    num = jnp.where(first, outs[0], outs[1])
    den = pltpu.roll(jnp.where(first, outs[1], outs[0]), HD, 1)
    lse = jnp.where(first, tops[0], tops[1]) + jnp.log(den)
    turned = lse.T
    return (num / den).astype(BF), turned[0:1], turned[HD : HD + 1]


def attention_forward_kernel(len_ref, q_ref, k_ref, v_ref, ctx_ref, lse_ref):
    ctx, low, high = forward_pair(len_ref[pl.program_id(0)], q_ref[...], k_ref[...], v_ref[...])
    ctx_ref[...] = ctx
    lse_ref[0, 0, 0:1, :] = low
    lse_ref[0, 0, 1:2, :] = high


def attention_forward(lengths, qkv, seqs, length, width):
    pairs = width // PAIR
    return pl.pallas_call(
        attention_forward_kernel,
        grid_spec=pltpu.PrefetchScalarGridSpec(
            num_scalar_prefetch=1,
            grid=(seqs, pairs),
            in_specs=[
                pl.BlockSpec((length, PAIR), lambda s, p, n: (s, p)),
                pl.BlockSpec((length, PAIR), lambda s, p, n: (s, pairs + p)),
                pl.BlockSpec((length, PAIR), lambda s, p, n: (s, 2 * pairs + p)),
            ],
            out_specs=[
                pl.BlockSpec((length, PAIR), lambda s, p, n: (s, p)),
                pl.BlockSpec((1, 1, 2, length), lambda s, p, n: (s, p, 0, 0)),
            ],
        ),
        out_shape=[
            jax.ShapeDtypeStruct((seqs * length, width), BF),
            jax.ShapeDtypeStruct((seqs, pairs, 2, length), F32),
        ],
        name="attention_forward",
    )(lengths, qkv, qkv, qkv)


def backward_pair(valid, q2, k2, v2, g2, ctx2, lses):
    lane = head_masks(q2.shape[0])
    first = lane < HD
    q2 = q2 * BF(0.125)
    k8 = k2 * BF(0.125)
    turned = (g2.astype(F32) * ctx2.astype(F32)).T
    dqs, dks, dvs = [], [], []
    for h in (0, 1):
        km = masked_keys(k2, lane, h, valid)
        qm = masked_query(q2, lane, h)
        vm = jnp.where((lane // HD) == h, v2, jnp.zeros_like(v2))
        delta = jnp.sum(turned[h * HD : (h + 1) * HD], axis=0, keepdims=True)
        p = jnp.exp(nt(km, qm) - lses[h])
        ds = (p * (nt(vm, g2) - delta)).astype(BF)
        dvs.append(nn(p.astype(BF), g2))
        dks.append(nn(ds, q2))
        dqs.append(tn(ds, k8))
    return [jnp.where(first, pair[0], pair[1]).astype(BF) for pair in (dqs, dks, dvs)]


def attention_backward_kernel(len_ref, q_ref, k_ref, v_ref, g_ref, ctx_ref, lse_ref, dq_ref, dk_ref, dv_ref):
    lses = [lse_ref[0, 0, h : h + 1, :] for h in (0, 1)]
    valid = len_ref[pl.program_id(0)]
    dq_ref[...], dk_ref[...], dv_ref[...] = backward_pair(
        valid, q_ref[...], k_ref[...], v_ref[...], g_ref[...], ctx_ref[...], lses
    )


def attention_backward(lengths, qkv, grad, ctx, lse, seqs, length, width):
    pairs = width // PAIR
    col = lambda k: pl.BlockSpec((length, PAIR), lambda s, p, n: (s, k * pairs + p))
    return pl.pallas_call(
        attention_backward_kernel,
        grid_spec=pltpu.PrefetchScalarGridSpec(
            num_scalar_prefetch=1,
            grid=(seqs, pairs),
            in_specs=[col(0), col(1), col(2), col(0), col(0), pl.BlockSpec((1, 1, 2, length), lambda s, p, n: (s, p, 0, 0))],
            out_specs=[col(0), col(0), col(0)],
        ),
        out_shape=[jax.ShapeDtypeStruct((seqs * length, width), BF)] * 3,
        name="attention_backward",
    )(lengths, qkv, qkv, qkv, grad, ctx, lse)


def neighbours():
    f, z = lax.axis_index("fsdp"), lax.axis_index("rep")
    core, x, y = f % 2, (f // 2) % 2, f // 4
    across_core = f + 1 - 2 * core
    step_x, step_y = 2 * (1 - 2 * x), 4 * (1 - 2 * y)
    return f, z, across_core, step_x, step_y


def remote(src, dst, send_sem, recv_sem, device):
    return pltpu.make_async_remote_copy(
        src_ref=src,
        dst_ref=dst,
        send_sem=send_sem,
        recv_sem=recv_sem,
        device_id=device,
        device_id_type=pl.DeviceIdType.MESH,
    )


def meet(depth, f, z, across_core, step_x, step_y):
    barrier = pltpu.get_barrier_semaphore()

    def greet(device):
        pl.semaphore_signal(barrier, inc=1, device_id=device, device_id_type=pl.DeviceIdType.MESH)

    for other in (across_core, f + step_x, f + step_y):
        greet((other, z))

    @pl.when(z > 0)
    def _():
        greet((f, z - 1))

    @pl.when(z < depth - 1)
    def _():
        greet((f, z + 1))

    pl.semaphore_wait(barrier, 3 + jnp.minimum(z, 1) + jnp.minimum(depth - 1 - z, 1))


def far_first(step, z):
    zero = 3 * (1 - z // 2)
    one = (2 + 3 * z) % 5
    two = 1 + z % 2
    picks = (zero, one, two, z)
    total = 0
    for i, pick in enumerate(picks):
        hit = 1 - jnp.minimum(jnp.abs(step - i), 1)
        total = total + hit * pick
    return total


def strips_of(arrays):
    found = []
    for index, array in enumerate(arrays):
        columns = array[1]
        if columns % 256 == 0:
            found.append((index, 0, columns // 2, True))
            found.append((index, columns // 2, columns // 2, False))
        else:
            found.append((index, 0, None, True))
    return found


def cut(ref, strip):
    if strip[2] is None:
        return ref
    return ref.at[:, pl.ds(strip[1], strip[2])]


def gather_parts(depth, strips, ins, outs, sems):
    count = len(ins)
    (own_sem, up_sem, down_sem, first_sem, second_sem, relay_sem, core_sem) = sems[:7]
    (got_column, got_first, got_second, got_diagonal, got_core) = sems[7:]
    f, z, across_core, step_x, step_y = neighbours()

    def slot(who, plane):
        return who * depth + plane

    def place(n, who, plane):
        return cut(outs[strips[n][0]].at[slot(who, plane)], strips[n])

    def toward(n):
        return (step_x, step_y) if strips[n][3] else (step_y, step_x)

    def own_copy(a):
        return pltpu.make_async_copy(ins[a], outs[a].at[slot(f, z)], own_sem.at[a])

    def core_copy(n, kind, plane, src):
        first, second = toward(n)
        who = f + (0, first, second, first + second)[kind]
        where = place(n, who, plane)
        return remote(where if src is None else src, where, core_sem.at[n, kind, plane], got_core.at[n, kind, plane], (across_core, z))

    def core_arrival(n, kind, plane):
        first, second = toward(n)
        who = across_core + (0, first, second, first + second)[kind]
        where = place(n, who, plane)
        return remote(where, where, core_sem.at[n, kind, plane], got_core.at[n, kind, plane], (across_core, z))

    def column_up(n, plane, src):
        return remote(src, place(n, f, plane), up_sem.at[n, plane], got_column.at[n, plane], (f, z + 1))

    def column_down(n, plane, src):
        return remote(src, place(n, f, plane), down_sem.at[n, plane], got_column.at[n, plane], (f, z - 1))

    def to_first(n, plane, src):
        return remote(src, place(n, f, plane), first_sem.at[n, plane], got_first.at[n, plane], (f + toward(n)[0], z))

    def to_second(n, plane, src):
        return remote(src, place(n, f, plane), second_sem.at[n, plane], got_second.at[n, plane], (f + toward(n)[1], z))

    def relay(n, plane):
        where = place(n, f + toward(n)[0], plane)
        return remote(where, where, relay_sem.at[n, plane], got_diagonal.at[n, plane], (f + toward(n)[1], z))

    def each(body):
        for n in range(len(strips)):
            body(n)

    def send_own(n):
        src = cut(ins[strips[n][0]], strips[n])
        to_first(n, z, src).start()
        to_second(n, z, src).start()

        @pl.when(z < depth - 1)
        def _():
            column_up(n, z, src).start()

        @pl.when(z > 0)
        def _():
            column_down(n, z, src).start()

        core_copy(n, 0, z, src).start()

    def begin():
        meet(depth, f, z, across_core, step_x, step_y)
        for a in range(count):
            own_copy(a).start()
        each(send_own)

    def phase(t):
        plane = far_first(depth - 1 - t, z)
        before = far_first(depth - t, z)
        earlier = far_first(depth + 1 - t, z)

        @pl.when((t >= 1) & (t < depth))
        def _():
            def arrived(n):
                src = place(n, f, plane)
                remote(src, src, up_sem.at[n, plane], got_column.at[n, plane], (f, z)).wait_recv()
                to_first(n, plane, src).start()
                to_second(n, plane, src).start()

                @pl.when((plane < z) & (z < depth - 1))
                def _():
                    column_up(n, plane, src).start()

                @pl.when((plane > z) & (z > 0))
                def _():
                    column_down(n, plane, src).start()

                core_copy(n, 0, plane, None).start()

            each(arrived)

        @pl.when((t >= 1) & (t < depth + 1))
        def _():
            def beside(n):
                first, second = toward(n)
                here = place(n, f + first, before)
                remote(here, here, first_sem.at[n, before], got_first.at[n, before], (f + first, z)).wait_recv()
                relay(n, before).start()
                core_copy(n, 1, before, None).start()

            each(beside)

            def above(n):
                first, second = toward(n)
                here = place(n, f + second, before)
                remote(here, here, second_sem.at[n, before], got_second.at[n, before], (f + second, z)).wait_recv()
                core_copy(n, 2, before, None).start()

            each(above)

        @pl.when(t >= 2)
        def _():
            def opposite(n):
                first, second = toward(n)
                here = place(n, f + first + second, earlier)
                remote(here, here, relay_sem.at[n, earlier], got_diagonal.at[n, earlier], (f + second, z)).wait_recv()
                core_copy(n, 3, earlier, None).start()

            each(opposite)

    def close_plane(plane, carry):
        def close(n):
            src = place(n, f, plane)
            to_first(n, plane, src).wait_send()
            to_second(n, plane, src).wait_send()
            relay(n, plane).wait_send()

            @pl.when((plane <= z) & (z < depth - 1))
            def _():
                column_up(n, plane, src).wait_send()

            @pl.when((plane >= z) & (z > 0))
            def _():
                column_down(n, plane, src).wait_send()

            for kind in range(4):
                core_copy(n, kind, plane, None).wait_send()
                core_arrival(n, kind, plane).wait_recv()

        each(close)
        return carry

    def finish():
        for a in range(count):
            own_copy(a).wait()
        lax.fori_loop(0, depth, close_plane, 0)

    return begin, phase, finish


def gather_kernel(depth, strips, count, *refs):
    ins, outs, sems = refs[:count], refs[count : 2 * count], refs[2 * count :]
    begin, phase, finish = gather_parts(depth, strips, ins, outs, sems)
    begin()

    def step(t, carry):
        phase(t)
        return carry

    lax.fori_loop(1, depth + 2, step, 0)
    finish()


def gather_semaphores(strips, count, depth):
    dma = pltpu.SemaphoreType.DMA
    flat, cored = dma((len(strips), depth)), dma((len(strips), 4, depth))
    return [dma((count,)), flat, flat, flat, flat, flat, cored, flat, flat, flat, flat, cored]


def gather_remote(mesh_shape, pieces):
    depth, devices = mesh_shape["rep"], mesh_shape["rep"] * mesh_shape["fsdp"]
    strips = strips_of([p.shape for p in pieces])
    count = len(pieces)
    return pl.pallas_call(
        functools.partial(gather_kernel, depth, strips, count),
        out_shape=[jax.ShapeDtypeStruct((devices,) + p.shape, p.dtype) for p in pieces],
        in_specs=[pl.BlockSpec(memory_space=pltpu.VMEM)] * count,
        out_specs=[pl.BlockSpec(memory_space=pl.ANY)] * count,
        scratch_shapes=gather_semaphores(strips, count, depth),
        compiler_params=pltpu.CompilerParams(collective_id=1, has_side_effects=True),
        name="gather_weights",
    )(*pieces)


def fits(mesh_shape, share):
    return mesh_shape["fsdp"] == 8 and mesh_shape["rep"] == 4 and share % 8 == 0


def gather(mesh_shape, pieces):
    if fits(mesh_shape, pieces[1].shape[0]):
        return gather_remote(mesh_shape, pieces)
    return gather_native(pieces)


def reduce_parts(depth, strips, terms, outs, scratch):
    count = len(terms)
    mine, theirs, relayed, direct, partial, below, above = (scratch[i * count : (i + 1) * count] for i in range(7))
    sems = scratch[7 * count :]
    (own_sem, core_sem, relay_sem, direct_sem, partial_sem, up_sem, down_sem) = sems[:7]
    (got_core, got_relay, got_direct, got_partial, got_below, got_above) = sems[7:]
    f, z, across_core, step_x, step_y = neighbours()

    def toward(n):
        return (step_x, step_y) if strips[n][3] else (step_y, step_x)

    def steps(n):
        first, second = toward(n)
        return (0, first, second, first + second)

    def term(n, who, plane):
        return cut(terms[strips[n][0]].at[who * depth + plane], strips[n])

    def cell(family, n, *index):
        return cut(family[strips[n][0]].at[index], strips[n])

    def own_copy(n, kind, plane):
        return pltpu.make_async_copy(term(n, f + steps(n)[kind], plane), cell(mine, n, kind, plane), own_sem.at[n, kind, plane])

    def core_copy(n, kind, plane):
        return remote(
            term(n, across_core + steps(n)[kind], plane),
            cell(theirs, n, kind, plane),
            core_sem.at[n, kind, plane],
            got_core.at[n, kind, plane],
            (across_core, z),
        )

    def relay(n, plane):
        return remote(cell(theirs, n, 3, plane), cell(relayed, n, plane), relay_sem.at[n, plane], got_relay.at[n, plane], (f + toward(n)[1], z))

    def straight(n, plane):
        return remote(cell(theirs, n, 2, plane), cell(direct, n, plane), direct_sem.at[n, plane], got_direct.at[n, plane], (f + toward(n)[1], z))

    def second_hop(n, plane):
        return remote(cell(theirs, n, 1, plane), cell(partial, n, plane), partial_sem.at[n, plane], got_partial.at[n, plane], (f + toward(n)[0], z))

    def go_up(n, plane):
        return remote(cell(theirs, n, 0, plane), cell(below, n, plane), up_sem.at[n, plane], got_below.at[n, plane], (f, z + 1))

    def go_down(n, plane):
        return remote(cell(theirs, n, 0, plane), cell(above, n, plane), down_sem.at[n, plane], got_above.at[n, plane], (f, z - 1))

    def add(n, kind, plane, *others):
        here = cell(theirs, n, kind, plane)
        total = here[...].astype(F32)
        for other in others:
            total = total + other[...].astype(F32)
        here[...] = total.astype(here.dtype)

    each = range(len(strips))
    order = (3, 2, 1, 0)

    def launch(t, carry):
        plane = far_first(t, z)
        for kind in order:
            for n in each:
                core_copy(n, kind, plane).start()
                own_copy(n, kind, plane).start()
        return carry

    def begin():
        meet(depth, f, z, across_core, step_x, step_y)
        lax.fori_loop(0, depth, launch, 0)

    def phase(t):
        plane = far_first(t, z)
        before = far_first(t - 1, z)
        earlier = far_first(t - 2, z)

        @pl.when(t < depth)
        def _():
            for kind in order:
                for n in each:
                    core_copy(n, kind, plane).wait_recv()
                    own_copy(n, kind, plane).wait()
                    add(n, kind, plane, cell(mine, n, kind, plane))
                if kind == 3:
                    for n in each:
                        relay(n, plane).start()
                if kind == 2:
                    for n in each:
                        straight(n, plane).start()

        @pl.when((t >= 1) & (t < depth + 1))
        def _():
            for n in each:
                relay(n, before).wait_recv()
                add(n, 1, before, cell(relayed, n, before))
            for n in each:
                second_hop(n, before).start()

        @pl.when(t >= 2)
        def _():
            for n in each:
                straight(n, earlier).wait_recv()
                second_hop(n, earlier).wait_recv()
                add(n, 0, earlier, cell(direct, n, earlier), cell(partial, n, earlier))

            @pl.when((earlier >= z) & (z > 0))
            def _():
                for n in each:
                    go_up(n, earlier).wait_recv()
                    add(n, 0, earlier, cell(below, n, earlier))

            @pl.when((earlier <= z) & (z < depth - 1))
            def _():
                for n in each:
                    go_down(n, earlier).wait_recv()
                    add(n, 0, earlier, cell(above, n, earlier))

            @pl.when(earlier > z)
            def _():
                for n in each:
                    go_up(n, earlier).start()

            @pl.when(earlier < z)
            def _():
                for n in each:
                    go_down(n, earlier).start()

    def close_plane(plane, carry):
        for n in each:
            for kind in order:
                core_copy(n, kind, plane).wait_send()
            relay(n, plane).wait_send()
            straight(n, plane).wait_send()
            second_hop(n, plane).wait_send()

        @pl.when(plane > z)
        def _():
            for n in each:
                go_up(n, plane).wait_send()

        @pl.when(plane < z)
        def _():
            for n in each:
                go_down(n, plane).wait_send()

        return carry

    def finish():
        for a in range(count):
            outs[a][...] = theirs[a][0, z].astype(F32)
        lax.fori_loop(0, depth, close_plane, 0)

    return begin, phase, finish


def reduce_kernel(depth, strips, count, *refs):
    terms, outs, scratch = refs[:count], refs[count : 2 * count], refs[2 * count :]
    begin, phase, finish = reduce_parts(depth, strips, terms, outs, scratch)
    begin()

    def step(t, carry):
        phase(t)
        return carry

    lax.fori_loop(0, depth + 2, step, 0)
    finish()


def reduce_scratch(terms, strips, depth):
    dma = pltpu.SemaphoreType.DMA
    flat, cored = dma((len(strips), depth)), dma((len(strips), 4, depth))
    whole = [pltpu.VMEM((4, depth) + t.shape[1:], t.dtype) for t in terms]
    line = [pltpu.VMEM((depth,) + t.shape[1:], t.dtype) for t in terms]
    return whole + whole + line * 5 + [cored, cored, flat, flat, flat, flat, flat, cored, flat, flat, flat, flat, flat]


def reduce_remote(mesh_shape, terms, collective_id=2):
    depth = mesh_shape["rep"]
    strips = strips_of([t.shape[1:] for t in terms])
    count = len(terms)
    return pl.pallas_call(
        functools.partial(reduce_kernel, depth, strips, count),
        out_shape=[jax.ShapeDtypeStruct(t.shape[1:], F32) for t in terms],
        in_specs=[pl.BlockSpec(memory_space=pl.ANY)] * count,
        out_specs=[pl.BlockSpec(memory_space=pltpu.VMEM)] * count,
        scratch_shapes=reduce_scratch(terms, strips, depth),
        compiler_params=pltpu.CompilerParams(
            collective_id=collective_id, has_side_effects=True, vmem_limit_bytes=48 * 1024 * 1024
        ),
        name="reduce_terms",
    )(*terms)


def reduce(mesh_shape, terms):
    if fits(mesh_shape, terms[1].shape[1]):
        return reduce_remote(mesh_shape, [t.astype(F32 if i == 0 else BF) for i, t in enumerate(terms)])
    return reduce_native(terms)


def lane_block(index, size):
    return pl.ds(pl.multiple_of(index * size, size), size)


def forward_kernel(depth, strips, count, heads_at_once, len_ref, x_ref, w_ref, b_ref, *refs):
    ins, refs = refs[:count], refs[count:]
    qkv_ref, ctx_ref, lse_ref = refs[:3]
    outs, sems = refs[3 : 3 + count], refs[3 + count :]
    begin, phase, finish = gather_parts(depth, strips, ins, outs, sems)
    width = x_ref.shape[1]
    seqs = len_ref.shape[0]
    length = x_ref.shape[0] // seqs
    block = heads_at_once * PAIR
    begin()

    def step(t, carry):
        j = t // 2

        @pl.when(t % 2 == 0)
        def _():
            for part in range(3):
                columns = pl.ds(pl.multiple_of(part * width + j * block, block), block)
                qkv_ref[:, columns] = (nn(x_ref[...], w_ref[:, columns]) + b_ref[:, columns]).astype(BF)

        @pl.when(t % 2 == 1)
        def _():
            def attend(i, inner):
                s, p = i // heads_at_once, j * heads_at_once + i % heads_at_once
                rows = lane_block(s, length)
                q2, k2, v2 = (
                    qkv_ref[rows, pl.ds(pl.multiple_of(part * width + p * PAIR, PAIR), PAIR)] for part in range(3)
                )
                ctx, low, high = forward_pair(len_ref[s], q2, k2, v2)
                ctx_ref[rows, lane_block(p, PAIR)] = ctx
                lse_ref[s, p, 0:1, :] = low
                lse_ref[s, p, 1:2, :] = high
                return inner

            lax.fori_loop(0, seqs * heads_at_once, attend, 0)

        @pl.when(t >= 1)
        def _():
            phase(t)

        return carry

    lax.fori_loop(0, depth + 2, step, 0)
    finish()


def forward_and_gather(mesh_shape, lengths, inputs, w_qkv, b_qkv, pieces, collective_id=3):
    depth, devices = mesh_shape["rep"], mesh_shape["rep"] * mesh_shape["fsdp"]
    strips = strips_of([p.shape for p in pieces])
    count = len(pieces)
    rows, width = inputs.shape
    seqs = lengths.shape[0]
    pairs = width // PAIR
    vmem = pl.BlockSpec(memory_space=pltpu.VMEM)
    out = pl.pallas_call(
        functools.partial(forward_kernel, depth, strips, count, pairs * 2 // (depth + 2)),
        out_shape=[
            jax.ShapeDtypeStruct((rows, 3 * width), BF),
            jax.ShapeDtypeStruct((rows, width), BF),
            jax.ShapeDtypeStruct((seqs, pairs, 2, rows // seqs), F32),
        ]
        + [jax.ShapeDtypeStruct((devices,) + p.shape, p.dtype) for p in pieces],
        in_specs=[pl.BlockSpec(memory_space=pltpu.SMEM)] + [vmem] * (3 + count),
        out_specs=[vmem] * 3 + [pl.BlockSpec(memory_space=pl.ANY)] * count,
        scratch_shapes=gather_semaphores(strips, count, depth),
        compiler_params=pltpu.CompilerParams(
            collective_id=collective_id, has_side_effects=True, vmem_limit_bytes=48 * 1024 * 1024
        ),
        name="forward_and_gather",
    )(lengths, inputs, w_qkv, b_qkv.reshape(1, 3 * width), *pieces)
    return out[0], out[1], out[2], out[3:]


def backward_kernel(depth, strips, count, heads_at_once, len_ref, x_ref, w_ref, qkv_ref, g_ref, ctx_ref, lse_ref, sum_ref, *refs):
    terms, refs = refs[:count], refs[count:]
    dw_ref, dx_ref, bias_ref = refs[:3]
    outs, refs = refs[3 : 3 + count], refs[3 + count :]
    dqkv_ref, total_ref, scratch = refs[0], refs[1], refs[2:]
    begin, phase, finish = reduce_parts(depth, strips, terms, outs, scratch)
    width = x_ref.shape[1]
    seqs = len_ref.shape[0]
    length = x_ref.shape[0] // seqs
    block = heads_at_once * PAIR
    begin()
    total_ref[...] = sum_ref[...]

    def step(t, carry):
        j = t // 2

        @pl.when(t % 2 == 0)
        def _():
            def attend(i, inner):
                s, p = i // heads_at_once, j * heads_at_once + i % heads_at_once
                rows = lane_block(s, length)
                places = [pl.ds(pl.multiple_of(part * width + p * PAIR, PAIR), PAIR) for part in range(3)]
                own = lane_block(p, PAIR)
                q2, k2, v2 = (qkv_ref[rows, place] for place in places)
                lses = [lse_ref[s, p, h : h + 1, :] for h in (0, 1)]
                grads = backward_pair(len_ref[s], q2, k2, v2, g_ref[rows, own], ctx_ref[rows, own], lses)
                for place, grad in zip(places, grads):
                    dqkv_ref[rows, place] = grad
                return inner

            lax.fori_loop(0, seqs * heads_at_once, attend, 0)

        @pl.when(t % 2 == 1)
        def _():
            for part in range(3):
                columns = pl.ds(pl.multiple_of(part * width + j * block, block), block)
                grad = dqkv_ref[:, columns]
                dw_ref[:, columns] = tn(x_ref[...], grad).astype(BF)
                bias_ref[:, columns] = jnp.sum(grad.astype(F32), axis=0, keepdims=True)
                total_ref[...] += nt(grad, w_ref[:, columns])

        phase(t)
        return carry

    lax.fori_loop(0, depth + 2, step, 0)
    dx_ref[...] = total_ref[...].astype(BF)
    finish()


def backward_and_reduce(mesh_shape, lengths, inputs, w_qkv, qkv, grad, ctx, lse, grad_sum, terms, collective_id=4):
    depth = mesh_shape["rep"]
    strips = strips_of([t.shape[1:] for t in terms])
    count = len(terms)
    rows, width = inputs.shape
    pairs = width // PAIR
    vmem = pl.BlockSpec(memory_space=pltpu.VMEM)
    out = pl.pallas_call(
        functools.partial(backward_kernel, depth, strips, count, pairs * 2 // (depth + 2)),
        out_shape=[
            jax.ShapeDtypeStruct((width, 3 * width), BF),
            jax.ShapeDtypeStruct((rows, width), BF),
            jax.ShapeDtypeStruct((1, 3 * width), F32),
        ]
        + [jax.ShapeDtypeStruct(t.shape[1:], F32) for t in terms],
        in_specs=[pl.BlockSpec(memory_space=pltpu.SMEM)] + [vmem] * 7 + [pl.BlockSpec(memory_space=pl.ANY)] * count,
        out_specs=[vmem] * (3 + count),
        scratch_shapes=[pltpu.VMEM((rows, 3 * width), BF), pltpu.VMEM((rows, width), F32)] + reduce_scratch(terms, strips, depth),
        compiler_params=pltpu.CompilerParams(
            collective_id=collective_id, has_side_effects=True, vmem_limit_bytes=63 * 1024 * 1024
        ),
        name="backward_and_reduce",
    )(lengths, inputs, w_qkv, qkv, grad, ctx, lse, grad_sum, *terms)
    return out[0], out[1], out[2], out[3:]


def norm_stats(hidden):
    mean = jnp.mean(hidden, axis=-1, keepdims=True)
    centred = hidden - mean
    inverse = lax.rsqrt(jnp.mean(centred * centred, axis=-1, keepdims=True) + EPS)
    return centred * inverse, inverse


def norm_pull(grad_normed, normed, inverse):
    return inverse * (
        grad_normed
        - jnp.mean(grad_normed, axis=-1, keepdims=True)
        - normed * jnp.mean(grad_normed * normed, axis=-1, keepdims=True)
    )


def total_rows(value):
    return jnp.sum(value.astype(F32), axis=0, keepdims=True)


def middle_kernel(depth, strips, x_ref, ctx_ref, cot_ref, w_out_ref, w_up_ref, w_down_ref, vec_ref, b_up_ref, *refs):
    hidden_ref, sum_ref, grad_ctx_ref, dw_out_ref, dw_up_ref, vec_out_ref, b_up_out_ref, owned_ref = refs[:8]
    active_ref, slope_ref, low_ref, normed_ref, inverse_ref, branch_ref, terms_ref = refs[8:15]
    begin, phase, finish = reduce_parts(depth, strips, (terms_ref,), (owned_ref,), refs[15:])
    rows, width = x_ref.shape
    hidden = w_up_ref.shape[1]
    chunk, block = 256, 256

    def vector(i):
        return vec_ref[i : i + 1, :]

    def put(i, value):
        vec_out_ref[i : i + 1, :] += value

    vec_out_ref[...] = jnp.zeros_like(vec_out_ref)

    def attention_out(i, carry):
        part = lane_block(i, chunk)
        first_sum = x_ref[part, :].astype(F32) + nn(ctx_ref[part, :], w_out_ref[...]) + vector(2)
        normed, inverse = norm_stats(first_sum)
        first = normed * vector(4) + vector(5)
        normed_ref[part, :] = normed
        inverse_ref[part, :] = inverse
        sum_ref[part, :] = first
        low_ref[part, :] = first.astype(BF)
        return carry

    lax.fori_loop(0, rows // chunk, attention_out, 0)

    def up(j, carry):
        columns = lane_block(j, block)
        inner = nn(low_ref[...], w_up_ref[:, columns]) + b_up_ref[:, columns]
        half = 0.5 + 0.5 * lax.erf(inner * (2.0**-0.5))
        active_ref[:, columns] = (inner * half).astype(BF)
        slope_ref[:, columns] = (half + inner * ((2.0 * math.pi) ** -0.5) * jnp.exp(-0.5 * inner * inner)).astype(BF)
        return carry

    lax.fori_loop(0, hidden // block, up, 0)

    def down(i, carry):
        part = lane_block(i, chunk)
        second_sum = sum_ref[part, :] + nn(active_ref[part, :], w_down_ref[...]) + vector(3)
        normed, inverse = norm_stats(second_sum)
        hidden_ref[part, :] = (normed * vector(6) + vector(7)).astype(BF)
        grad_out = cot_ref[part, :].astype(F32)
        put(6, total_rows(grad_out * normed))
        put(7, total_rows(grad_out))
        grad_second = norm_pull(grad_out * vector(6), normed, inverse)
        sum_ref[part, :] = grad_second
        branch = grad_second.astype(BF)
        branch_ref[part, :] = branch
        put(3, total_rows(branch))
        return carry

    lax.fori_loop(0, rows // chunk, down, 0)

    share = terms_ref.shape[1]
    slots = 4

    def down_terms(i, carry):
        term = tn(active_ref[:, lane_block(i, slots * share)], branch_ref[...])
        terms_ref[pl.ds(i * slots, slots)] = term.astype(BF).reshape(slots, share, width)
        return carry

    lax.fori_loop(0, terms_ref.shape[0] // slots, down_terms, 0)
    begin()
    blocks = hidden // block
    stride = blocks // depth

    def up_back(j, carry):
        columns = lane_block(j, block)
        grad_active = nt(branch_ref[...], w_down_ref[columns, :])
        grad_inner = (grad_active * slope_ref[:, columns].astype(F32)).astype(BF)
        slope_ref[:, columns] = grad_inner
        b_up_out_ref[:, columns] = total_rows(grad_inner)
        dw_up_ref[:, columns] = tn(low_ref[...], grad_inner).astype(BF)

        @pl.when(j % stride == stride - 1)
        def _():
            phase(j // stride)

        return carry

    lax.fori_loop(0, blocks, up_back, 0)

    def first_back(i, carry):
        part = lane_block(i, chunk)
        grad_first = sum_ref[part, :] + nt(slope_ref[part, :], w_up_ref[...])
        normed = normed_ref[part, :]
        put(4, total_rows(grad_first * normed))
        put(5, total_rows(grad_first))
        grad = norm_pull(grad_first * vector(4), normed, inverse_ref[part, :])
        sum_ref[part, :] = grad
        low = grad.astype(BF)
        branch_ref[part, :] = low
        put(2, total_rows(low))
        grad_ctx_ref[part, :] = nt(low, w_out_ref[...]).astype(BF)
        return carry

    lax.fori_loop(0, rows // chunk, first_back, 0)
    dw_out_ref[...] = tn(ctx_ref[...], branch_ref[...]).astype(BF)
    lax.fori_loop(depth, depth + 2, lambda t, carry: (phase(t), carry)[1], 0)
    finish()


def middle(mesh_shape, inputs, context, cotangent, w_out, w_up, w_down, plain, b_up, collective_id=5):
    depth, devices = mesh_shape["rep"], mesh_shape["rep"] * mesh_shape["fsdp"]
    rows, width = inputs.shape
    hidden = w_up.shape[1]
    terms = jax.ShapeDtypeStruct((devices, hidden // devices, width), BF)
    strips = strips_of([terms.shape[1:]])
    vmem = pl.BlockSpec(memory_space=pltpu.VMEM)
    shape = jax.ShapeDtypeStruct
    return pl.pallas_call(
        functools.partial(middle_kernel, depth, strips),
        out_shape=[
            shape((rows, width), BF),
            shape((rows, width), F32),
            shape((rows, width), BF),
            shape((width, width), BF),
            shape((width, hidden), BF),
            shape((8, width), F32),
            shape((1, hidden), F32),
            shape(terms.shape[1:], F32),
        ],
        in_specs=[vmem] * 8,
        out_specs=[vmem] * 8,
        scratch_shapes=[
            pltpu.VMEM((rows, hidden), BF),
            pltpu.VMEM((rows, hidden), BF),
            pltpu.VMEM((rows, width), BF),
            pltpu.VMEM((rows, width), F32),
            pltpu.VMEM((rows, 1), F32),
            pltpu.VMEM((rows, width), BF),
            pltpu.VMEM(terms.shape, BF),
        ]
        + reduce_scratch([terms], strips, depth),
        compiler_params=pltpu.CompilerParams(
            collective_id=collective_id, has_side_effects=True, vmem_limit_bytes=67043328
        ),
        name="middle",
    )(inputs, context, cotangent, w_out, w_up, w_down, plain, b_up.reshape(1, hidden))

EPS = 1e-06
AXES = ("fsdp", "rep")


def norm_forward(hidden, gain, shift):
    mean = jnp.mean(hidden, axis=-1, keepdims=True)
    centred = hidden - mean
    inverse = lax.rsqrt(jnp.mean(centred * centred, axis=-1, keepdims=True) + EPS)
    normed = centred * inverse
    return (normed * gain + shift, normed, inverse)


def norm_backward(grad_out, normed, inverse, gain):
    grad_normed = grad_out * gain
    grad_in = inverse * (
        grad_normed
        - jnp.mean(grad_normed, axis=-1, keepdims=True)
        - normed * jnp.mean(grad_normed * normed, axis=-1, keepdims=True)
    )
    return (grad_in, jnp.sum(grad_out * normed, axis=0), jnp.sum(grad_out, axis=0))


def column_sums(grad):
    return jnp.sum(grad.astype(F32), axis=0)


def gather_native(pieces):
    return [lax.all_gather(p, AXES, axis=0, tiled=False) for p in pieces]


def reduce_native(terms):
    return [lax.psum_scatter(t.astype(F32), AXES, scatter_dimension=0, tiled=False) for t in terms]


def local(
    mesh_shape,
    hidden_in,
    lengths,
    query_weight,
    key_weight,
    value_weight,
    out_weight,
    up_weight,
    down_weight,
    query_bias,
    value_bias,
    out_bias,
    up_bias,
    down_bias,
    first_gain,
    first_shift,
    second_gain,
    second_shift,
    cotangent,
):
    seqs, length, width = hidden_in.shape
    rows = seqs * length
    hidden = up_weight.shape[1]
    share = query_weight.shape[0]
    spread = hidden // width
    devices = width // share
    vectors = jnp.concatenate(
        [
            jnp.stack([query_bias, value_bias, out_bias, down_bias, first_gain, first_shift, second_gain, second_shift]),
            up_bias.reshape(spread, share),
        ]
    )
    count = vectors.shape[0]
    vector_slot = jnp.pad(vectors, ((0, -count % 16), (0, -share % 128)))
    qkv_shard = jnp.concatenate([query_weight, key_weight, value_weight], axis=1)
    later = [out_weight, up_weight, down_weight]
    fused = fits(mesh_shape, share)
    got = gather(mesh_shape, [vector_slot, qkv_shard])
    w_qkv = got[1].reshape(width, 3 * width)
    wide = got[0].astype(F32)
    plain = jnp.transpose(wide[:, :8, :share], (1, 0, 2)).reshape(8, width)
    b_query, b_values, b_out, b_down, gain_one, shift_one, gain_two, shift_two = [plain[i] for i in range(8)]
    b_up = wide[:, 8 : 8 + spread, :share].reshape(hidden)

    inputs = hidden_in.reshape(rows, width)
    b_qkv = jnp.concatenate([b_query, jnp.zeros_like(b_query), b_values])
    if fused:
        qkv, context, log_sums, got = forward_and_gather(mesh_shape, lengths, inputs, w_qkv, b_qkv, later)
    else:
        got = gather(mesh_shape, later)
        qkv = (nn(inputs, w_qkv) + b_qkv).astype(BF)
        context, log_sums = attention_forward(lengths, qkv, seqs, length, width)
    w_out = got[0].reshape(width, width)
    w_up = got[1].reshape(width, hidden)
    w_down = got[2].reshape(hidden, width)
    if fused:
        hidden_out, grad_first_sum, grad_context, grad_w_out, grad_w_up, vector_sums, grad_b_up, owned_down = middle(
            mesh_shape, inputs, context, cotangent.reshape(rows, width), w_out, w_up, w_down, plain, b_up
        )
        hidden_out = hidden_out.reshape(seqs, length, width)
        later = [grad_w_out.reshape(devices, share, width), grad_w_up.reshape(devices, share, hidden)]
        grad_w_qkv, input_grad, bias_sums, owned_later = backward_and_reduce(
            mesh_shape, lengths, inputs, w_qkv, qkv, grad_context, context, log_sums, grad_first_sum, later
        )
        owned_later = [owned_later[0], owned_later[1], owned_down]
        bias_sums = bias_sums[0]
        sums = jnp.concatenate([jnp.stack([bias_sums[:width], bias_sums[2 * width :]]), vector_sums[2:]])
    else:
        first_sum = inputs.astype(F32) + nn(context, w_out) + b_out
        first, normed_one, inverse_one = norm_forward(first_sum, gain_one, shift_one)
        first_low = first.astype(BF)
        inner = nn(first_low, w_up) + b_up
        half = 0.5 * (1.0 + lax.erf(inner * (2.0**-0.5)))
        active = (inner * half).astype(BF)
        slope = half + inner * ((2.0 * math.pi) ** -0.5) * jnp.exp(-0.5 * inner * inner)
        slope = slope.astype(BF)
        second_sum = first + nn(active, w_down) + b_down
        result, normed_two, inverse_two = norm_forward(second_sum, gain_two, shift_two)
        hidden_out = result.astype(BF).reshape(seqs, length, width)
        grad_out = cotangent.reshape(rows, width).astype(F32)
        grad_second, grad_gain_two, grad_shift_two = norm_backward(grad_out, normed_two, inverse_two, gain_two)
        grad_branch = grad_second.astype(BF)
        grad_b_down = column_sums(grad_branch)
        grad_w_down = tn(active, grad_branch)
        grad_active = nt(grad_branch, w_down)
        grad_inner = (grad_active * slope.astype(F32)).astype(BF)
        grad_b_up = column_sums(grad_inner)
        grad_w_up = tn(first_low, grad_inner)
        grad_first = grad_second + nt(grad_inner, w_up)
        grad_first_sum, grad_gain_one, grad_shift_one = norm_backward(grad_first, normed_one, inverse_one, gain_one)
        grad_attn = grad_first_sum.astype(BF)
        grad_b_out = column_sums(grad_attn)
        grad_w_out = tn(context, grad_attn)
        grad_context = nt(grad_attn, w_out).astype(BF)
        later = [
            grad_w_out.reshape(devices, share, width),
            grad_w_up.reshape(devices, share, hidden),
            grad_w_down.reshape(devices, spread * share, width),
        ]
        grad_query, grad_keys, grad_values = attention_backward(
            lengths, qkv, grad_context, context, log_sums, seqs, length, width
        )
        grad_qkv = jnp.concatenate([grad_query, grad_keys, grad_values], axis=1)
        input_grad = (grad_first_sum + nt(grad_qkv, w_qkv)).astype(BF)
        grad_w_qkv = tn(inputs, grad_qkv)
        bias_sums = column_sums(grad_qkv)
        owned_later = reduce_native(later)
        sums = jnp.stack(
            [
                bias_sums[:width],
                bias_sums[2 * width :],
                grad_b_out,
                grad_b_down,
                grad_gain_one,
                grad_shift_one,
                grad_gain_two,
                grad_shift_two,
            ]
        )
    input_grad = input_grad.reshape(seqs, length, width)
    vector_terms = jnp.concatenate(
        [jnp.transpose(sums.reshape(8, devices, share), (1, 0, 2)), grad_b_up.reshape(devices, spread, share)], axis=1
    )
    vector_terms = jnp.pad(vector_terms, ((0, 0), (0, -count % 16), (0, -share % 128)))
    owned = reduce(mesh_shape, [vector_terms, grad_w_qkv.reshape(devices, share, 3 * width)])
    vec = owned[0][:count, :share]
    return (
        hidden_out,
        input_grad,
        owned[1][:, :width],
        owned[1][:, width : 2 * width],
        owned[1][:, 2 * width :],
        owned_later[0],
        owned_later[1],
        owned_later[2],
        vec[0],
        vec[1],
        vec[2],
        vec[8:].reshape(spread * share),
        vec[3],
        vec[4],
        vec[5],
        vec[6],
        vec[7],
    )


def solution(mesh):
    rows = P(AXES, None)
    flat = P(AXES)
    cube = P(AXES, None, None)
    in_specs = (cube, flat) + (rows,) * 6 + (flat,) * 9 + (cube,)
    out_specs = (cube, cube) + (rows,) * 6 + (flat,) * 9
    body = functools.partial(local, dict(mesh.shape))
    return jax.shard_map(body, mesh=mesh, in_specs=in_specs, out_specs=out_specs, check_vma=False)
```

profile of v0, /device:TPU:0, one launch (start us, length us, event | category | flops | bytes accessed | tf_op | source)
XLA Modules:
  0.0 279.4 jit_solution(5721516418554674350)
XLA Ops:
  0.7 1.5 pad_maximum_fusion.refs_1_
  2.1 0.7 reshape.95
  2.9 0.8 concatenate.22
  3.7 0.6 pad.8.refs_0_
  4.3 29.7 %gather_weights.1 = (bf16[32,16,128]{2,1,0:T(8,128)(2,1)}, bf16[32,24,2304]{2,1,0:T(8,128)(2,1)}) custom-call(bf16[16,128]{1,0:T(8,128)(2,1)} %pad.8.refs_0_, bf16[24,2304]{1,0:T(8,128)(2,1)} %pad_maximum_fusion.refs_1_), custom_call_target="tpu_custom_call" | custom-call | tf_op jit(solution)/shard_map/gather_weights/pallas_call | solution.py:389
  34.0 0.9 convert_element_type.7
  34.9 0.1 slice_reduce_fusion.1
  35.0 0.1 squeeze.31
  35.1 0.1 squeeze.32
  35.2 0.0 copy-start
  35.2 1.4 copy-done
  36.6 0.0 copy-start.4
  36.6 0.9 copy-done.4
  37.6 0.0 copy-start.5
  37.6 0.9 copy-done.5
  38.5 0.0 copy-start.7
  38.5 0.8 copy-done.7
  39.2 0.0 copy-start.8
  39.2 0.7 copy-done.8
  39.9 58.8 %forward_and_gather.1 = (bf16[1024,2304]{1,0:T(8,128)(2,1)}, bf16[1024,768]{1,0:T(8,128)(2,1)S(1)}, f32[2,6,2,512]{3,2,1,0:T(2,128)S(1)}, bf16[32,24,768]{2,1,0:...) custom-call(s32[2]{0:T(128)S(1)} %copy-done.8, bf16[1024,768]{1,0:T(8,128)(2,1)S(1)} %bitcast.43, ...), custom_call_target="tpu_custom_call" | custom-call | tf_op jit(solution)/shard_map/forward_and_gather/pallas_call | solution.py:666
  98.7 0.0 copy-start.1
  98.7 1.1 copy-done.1
  99.8 0.0 copy-start.3
  99.8 1.0 copy-done.3
  100.9 0.0 copy-start.6
  100.9 0.6 copy-done.6
  101.5 0.7 reshape.102.vec_ref
  102.2 0.0 copy-done.11
  102.2 0.7 reshape_reshape.3.b_up_ref
  103.0 80.0 %middle.1 = (bf16[1024,768]{1,0:T(8,128)(2,1)}, f32[1024,768]{1,0:T(8,128)}, bf16[1024,768]{1,0:T(8,128)(2,1)}, bf16[768,768]{1,0:T(8,128)(2,1)}, bf16[768,3072]...) custom-call(bf16[1024,768]{1,0:T(8,128)(2,1)} %bitcast.41, ...), custom_call_target="tpu_custom_call" | custom-call | tf_op jit(solution)/shard_map/middle/pallas_call | solution.py:892
  183.0 0.0 copy-start.15
  183.0 0.0 copy-start.16
  183.0 54.8 %backward_and_reduce.1 = (bf16[768,2304]{1,0:T(8,128)(2,1)}, bf16[1024,768]{1,0:T(8,128)(2,1)}, f32[1,2304]{1,0:T(1,128)}, f32[24,768]{1,0:T(8,128)}, f32[24,3072]{1,0:T(8,128)}) custom-call(s32[2]{0:T(128)} %len_ref.3, bf16[1024,768]{1,0:T(8,128)(2,1)} %bitcast.42, bf16[768,2304]{1,0:T(8,128)(2,1)} %bitcast.47, ...), custom_call_target="tpu_custom_call" | custom-call | tf_op jit(solution)/shard_map/backward_and_reduce/pallas_call | solution.py:741
  237.8 0.7 slice_reduce_fusion.3
  238.5 0.1 concatenate.25
  238.6 0.1 concatenate.26
  238.7 0.0 copy-done.15
  238.7 0.1 concatenate.27
  238.8 0.1 copy.39
  238.9 0.1 maximum_bitcast_fusion
  238.9 0.5 broadcast.26
  239.5 0.0 copy-done.16
  239.5 0.7 reduce.15
  240.1 0.1 reshape.107
  240.3 0.0 copy-start.2
  240.3 2.0 copy-done.2
  242.3 30.0 %reduce_terms.1 = (f32[16,128]{1,0:T(8,128)S(1)}, f32[24,2304]{1,0:T(8,128)S(1)}) custom-call(f32[32,16,128]{2,1,0:T(8,128)S(1)} %select_maximum_fusion.refs_0_, bf16[32,24,2304]{2,1,0:T(8,128)(2,1)S(1)} %bitcast.44), custom_call_target="tpu_custom_call" | custom-call | tf_op jit(solution)/shard_map/reduce_terms/pallas_call | solution.py:589
  272.4 0.7 fusion
  273.1 0.5 slice_bitcast_fusion.1
  273.6 0.6 reshape.109
  274.2 0.0 copy-done.9
  274.2 0.0 copy-start.10
  274.2 1.1 copy.45
  275.4 0.8 copy-done.10
  276.2 0.0 copy-start.14
  276.2 0.0 copy-start.13
  276.2 0.0 copy-start.12
  276.2 1.1 copy.46
  277.3 0.0 copy-done.14
  277.3 0.6 copy.47
  278.0 0.0 copy-done.13
  278.0 0.7 copy.48
  278.7 0.0 copy-done.12
  278.7 0.7 copy.49
  (11 shorter events, 0.1 us)
Async XLA Ops:
  35.2 1.4 copy-start
  36.6 0.9 copy-start.4
  37.6 0.9 copy-start.5
  38.5 0.8 copy-start.7
  39.2 0.7 copy-start.8
  39.9 62.3 %copy-start.11 = (bf16[32,16,128]{2,1,0:T(8,128)(2,1)S(1)}, bf16[32,16,128]{2,1,0:T(8,128)(2,1)}, u32[]{:S(2)}) copy-start(bf16[32,16,128]{2,1,0:T(8,128)(2,1)} %get-tuple-element.41) | copy-start | bytes 393220
  98.7 1.1 copy-start.1
  99.8 1.0 copy-start.3
  100.9 0.6 copy-start.6
  183.0 55.7 %copy-start.15 = (f32[8,768]{1,0:T(8,128)S(1)}, f32[8,768]{1,0:T(8,128)}, u32[]{:S(2)}) copy-start(f32[8,768]{1,0:T(8,128)} %get-tuple-element.55) | copy-start | bytes 73732
  183.0 56.5 %copy-start.16 = (f32[1,3072]{1,0:T(1,128)S(1)}, f32[1,3072]{1,0:T(1,128)}, u32[]{:S(2)}) copy-start(f32[1,3072]{1,0:T(1,128)} %get-tuple-element.56) | copy-start | bytes 36868
  240.3 2.0 copy-start.2
  242.3 31.9 %copy-start.9 = (bf16[1024,768]{1,0:T(8,128)(2,1)S(1)}, bf16[1024,768]{1,0:T(8,128)(2,1)}, u32[]{:S(2)}) copy-start(bf16[1024,768]{1,0:T(8,128)(2,1)} %get-tuple-element.46) | copy-start | bytes 4718596
  274.2 2.0 copy-start.10
  276.2 1.2 copy-start.14
  276.2 1.8 copy-start.13
  276.2 2.5 copy-start.12
where the time goes:
time: 280 us; the launch traced here: 279 us
  Pallas kernels  253 us (90%)
  local copies, waits for them, and re-layouts  22 us (8%)
  other arithmetic  3.17 us (1%)
    pallas_call x1, Pallas kernels, middle(): pl.pallas_call(functools.partial(middle_kernel, depth, strips), out_shape...  80 us
    pallas_call x1, Pallas kernels, forward_and_gather(): pl.pallas_call(functools.partial(forward_kernel, depth, strips, count, pa...  58.8 us
    pallas_call x1, Pallas kernels, backward_and_reduce(): pl.pallas_call(functools.partial(backward_kernel, depth, strips, count, p...  54.8 us
    pallas_call x1, Pallas kernels, reduce_remote(): pl.pallas_call(functools.partial(reduce_kernel, depth, strips, count), ou...  30 us
    pallas_call x1, Pallas kernels, gather_remote(): pl.pallas_call(functools.partial(gather_kernel, depth, strips, count), ou...  29.7 us
    unnamed x39, local copies, waits for them, and re-layouts  14.6 us

commit v1 on v0

--- a/solution.py
+++ b/solution.py
@@ -167,15 +167,9 @@
     for other in (across_core, f + step_x, f + step_y):
         greet((other, z))
 
-    @pl.when(z > 0)
-    def _():
-        greet((f, z - 1))
-
-    @pl.when(z < depth - 1)
-    def _():
-        greet((f, z + 1))
-
-    pl.semaphore_wait(barrier, 3 + jnp.minimum(z, 1) + jnp.minimum(depth - 1 - z, 1))
+    for hop in range(1, depth):
+        greet((f, (z + hop) % depth))
+    pl.semaphore_wait(barrier, 3 + depth - 1)
 
 
 def far_first(step, z):
@@ -273,8 +267,9 @@
 
         core_copy(n, 0, z, src).start()
 
-    def begin():
-        meet(depth, f, z, across_core, step_x, step_y)
+    def begin(greet=True):
+        if greet:
+            meet(depth, f, z, across_core, step_x, step_y)
         for a in range(count):
             own_copy(a).start()
         each(send_own)
@@ -363,48 +358,14 @@
     return begin, phase, finish
 
 
-def gather_kernel(depth, strips, count, *refs):
-    ins, outs, sems = refs[:count], refs[count : 2 * count], refs[2 * count :]
-    begin, phase, finish = gather_parts(depth, strips, ins, outs, sems)
-    begin()
-
-    def step(t, carry):
-        phase(t)
-        return carry
-
-    lax.fori_loop(1, depth + 2, step, 0)
-    finish()
-
-
 def gather_semaphores(strips, count, depth):
     dma = pltpu.SemaphoreType.DMA
     flat, cored = dma((len(strips), depth)), dma((len(strips), 4, depth))
     return [dma((count,)), flat, flat, flat, flat, flat, cored, flat, flat, flat, flat, cored]
 
 
-def gather_remote(mesh_shape, pieces):
-    depth, devices = mesh_shape["rep"], mesh_shape["rep"] * mesh_shape["fsdp"]
-    strips = strips_of([p.shape for p in pieces])
-    count = len(pieces)
-    return pl.pallas_call(
-        functools.partial(gather_kernel, depth, strips, count),
-        out_shape=[jax.ShapeDtypeStruct((devices,) + p.shape, p.dtype) for p in pieces],
-        in_specs=[pl.BlockSpec(memory_space=pltpu.VMEM)] * count,
-        out_specs=[pl.BlockSpec(memory_space=pl.ANY)] * count,
-        scratch_shapes=gather_semaphores(strips, count, depth),
-        compiler_params=pltpu.CompilerParams(collective_id=1, has_side_effects=True),
-        name="gather_weights",
-    )(*pieces)
-
-
 def fits(mesh_shape, share):
     return mesh_shape["fsdp"] == 8 and mesh_shape["rep"] == 4 and share % 8 == 0
-
-
-def gather(mesh_shape, pieces):
-    if fits(mesh_shape, pieces[1].shape[0]):
-        return gather_remote(mesh_shape, pieces)
-    return gather_native(pieces)
 
 
 def reduce_parts(depth, strips, terms, outs, scratch):
@@ -473,8 +434,9 @@
                 own_copy(n, kind, plane).start()
         return carry
 
-    def begin():
-        meet(depth, f, z, across_core, step_x, step_y)
+    def begin(greet=True):
+        if greet:
+            meet(depth, f, z, across_core, step_x, step_y)
         lax.fori_loop(0, depth, launch, 0)
 
     def phase(t):
@@ -561,25 +523,125 @@
     return begin, phase, finish
 
 
-def reduce_kernel(depth, strips, count, *refs):
-    terms, outs, scratch = refs[:count], refs[count : 2 * count], refs[2 * count :]
-    begin, phase, finish = reduce_parts(depth, strips, terms, outs, scratch)
-    begin()
-
-    def step(t, carry):
-        phase(t)
-        return carry
-
-    lax.fori_loop(0, depth + 2, step, 0)
-    finish()
-
-
 def reduce_scratch(terms, strips, depth):
     dma = pltpu.SemaphoreType.DMA
     flat, cored = dma((len(strips), depth)), dma((len(strips), 4, depth))
     whole = [pltpu.VMEM((4, depth) + t.shape[1:], t.dtype) for t in terms]
     line = [pltpu.VMEM((depth,) + t.shape[1:], t.dtype) for t in terms]
     return whole + whole + line * 5 + [cored, cored, flat, flat, flat, flat, flat, cored, flat, flat, flat, flat, flat]
+
+
+def lane_block(index, size):
+    return pl.ds(pl.multiple_of(index * size, size), size)
+
+
+def forward_kernel(depth, strips, counts, len_ref, x_ref, *refs):
+    early, later = counts
+    ins, refs = refs[: early + later], refs[early + later :]
+    qkv_ref, ctx_ref, lse_ref, vec_ref = refs[:4]
+    outs, sems = refs[4 : 4 + early + later], refs[4 + early + later :]
+    kinds = len(sems) // 2
+    first = gather_parts(depth, strips[0], ins[:early], outs[:early], sems[:kinds])
+    second = gather_parts(depth, strips[1], ins[early:], outs[early:], sems[kinds:])
+    slots_ref, w_ref = outs[:early]
+    rows, width = x_ref.shape
+    seqs = len_ref.shape[0]
+    length = rows // seqs
+    block = 2 * PAIR
+
+    first[0]()
+    second[0](greet=False)
+
+    def arrive(t, carry):
+        first[1](t)
+
+        @pl.when((t >= depth - 1) & (t <= depth))
+        def _():
+            second[1](t - depth + 2)
+
+        return carry
+
+    lax.fori_loop(1, depth + 2, arrive, 0)
+    first[2]()
+    vec_ref[...] = jnp.sum(slots_ref[...].astype(F32), axis=0)
+
+    def step(t, carry):
+        j = t // 2
+
+        @pl.when(t % 2 == 0)
+        def _():
+            for part in range(3):
+                columns = pl.ds(pl.multiple_of(part * width + j * block, block), block)
+                made = nn(x_ref[...], w_ref[:, :, columns].reshape(width, block))
+                if part != 1:
+                    made = made + vec_ref[part // 2 : part // 2 + 1, lane_block(j, block)]
+                qkv_ref[:, columns] = made.astype(BF)
+
+        @pl.when(t % 2 == 1)
+        def _():
+            def attend(i, inner):
+                s, p = i // 2, j * 2 + i % 2
+                part_rows = lane_block(s, length)
+                q2, k2, v2 = (
+                    qkv_ref[part_rows, pl.ds(pl.multiple_of(part * width + p * PAIR, PAIR), PAIR)] for part in range(3)
+                )
+                ctx, low, high = forward_pair(len_ref[s], q2, k2, v2)
+                ctx_ref[part_rows, lane_block(p, PAIR)] = ctx
+                lse_ref[s, p, 0:1, :] = low
+                lse_ref[s, p, 1:2, :] = high
+                return inner
+
+            lax.fori_loop(0, seqs * 2, attend, 0)
+
+        @pl.when(t % 2 == 0)
+        def _():
+            second[1](depth - 1 + j)
+
+        return carry
+
+    lax.fori_loop(0, depth + 2, step, 0)
+    second[2]()
+
+
+def forward_and_gather(mesh_shape, lengths, inputs, early, later, collective_id=3):
+    depth, devices = mesh_shape["rep"], mesh_shape["rep"] * mesh_shape["fsdp"]
+    strips = [strips_of([p.shape for p in group]) for group in (early, later)]
+    counts = (len(early), len(later))
+    rows, width = inputs.shape
+    seqs = lengths.shape[0]
+    pairs = width // PAIR
+    vmem, away = pl.BlockSpec(memory_space=pltpu.VMEM), pl.BlockSpec(memory_space=pl.ANY)
+    out = pl.pallas_call(
+        functools.partial(forward_kernel, depth, strips, counts),
+        out_shape=[
+            jax.ShapeDtypeStruct((rows, 3 * width), BF),
+            jax.ShapeDtypeStruct((rows, width), BF),
+            jax.ShapeDtypeStruct((seqs, pairs, 2, rows // seqs), F32),
+            jax.ShapeDtypeStruct(early[0].shape, F32),
+        ]
+        + [jax.ShapeDtypeStruct((devices,) + p.shape, p.dtype) for p in early + later],
+        in_specs=[pl.BlockSpec(memory_space=pltpu.SMEM)] + [vmem] * (1 + sum(counts)),
+        out_specs=[vmem] * (4 + counts[0]) + [away] * counts[1],
+        scratch_shapes=gather_semaphores(strips[0], counts[0], depth) + gather_semaphores(strips[1], counts[1], depth),
+        compiler_params=pltpu.CompilerParams(
+            collective_id=collective_id, has_side_effects=True, vmem_limit_bytes=48 * 1024 * 1024
+        ),
+        name="forward_and_gather",
+    )(lengths, inputs, *early, *later)
+    return out[0], out[1], out[2], out[3], out[5], out[6:]
+
+
+def reduce_kernel(depth, strips, count, *refs):
+    terms, outs, scratch = refs[:count], refs[count : 2 * count], refs[2 * count :]
+    begin, phase, finish = reduce_parts(depth, strips, terms, outs, scratch)
+    begin()
+
+    def step(t, carry):
+        phase(t)
+        return carry
+
+    lax.fori_loop(0, depth + 2, step, 0)
+    finish()
 
 
 def reduce_remote(mesh_shape, terms, collective_id=2):
@@ -597,89 +659,6 @@
         ),
         name="reduce_terms",
     )(*terms)
-
-
-def reduce(mesh_shape, terms):
-    if fits(mesh_shape, terms[1].shape[1]):
-        return reduce_remote(mesh_shape, [t.astype(F32 if i == 0 else BF) for i, t in enumerate(terms)])
-    return reduce_native(terms)
-
-
-def lane_block(index, size):
-    return pl.ds(pl.multiple_of(index * size, size), size)
-
-
-def forward_kernel(depth, strips, count, heads_at_once, len_ref, x_ref, w_ref, b_ref, *refs):
-    ins, refs = refs[:count], refs[count:]
-    qkv_ref, ctx_ref, lse_ref = refs[:3]
-    outs, sems = refs[3 : 3 + count], refs[3 + count :]
-    begin, phase, finish = gather_parts(depth, strips, ins, outs, sems)
-    width = x_ref.shape[1]
-    seqs = len_ref.shape[0]
-    length = x_ref.shape[0] // seqs
-    block = heads_at_once * PAIR
-    begin()
-
-    def step(t, carry):
-        j = t // 2
-
-        @pl.when(t % 2 == 0)
-        def _():
-            for part in range(3):
-                columns = pl.ds(pl.multiple_of(part * width + j * block, block), block)
-                qkv_ref[:, columns] = (nn(x_ref[...], w_ref[:, columns]) + b_ref[:, columns]).astype(BF)
-
-        @pl.when(t % 2 == 1)
-        def _():
-            def attend(i, inner):
-                s, p = i // heads_at_once, j * heads_at_once + i % heads_at_once
-                rows = lane_block(s, length)
-                q2, k2, v2 = (
-                    qkv_ref[rows, pl.ds(pl.multiple_of(part * width + p * PAIR, PAIR), PAIR)] for part in range(3)
-                )
-                ctx, low, high = forward_pair(len_ref[s], q2, k2, v2)
-                ctx_ref[rows, lane_block(p, PAIR)] = ctx
-                lse_ref[s, p, 0:1, :] = low
-                lse_ref[s, p, 1:2, :] = high
-                return inner
-
-            lax.fori_loop(0, seqs * heads_at_once, attend, 0)
-
-        @pl.when(t >= 1)
-        def _():
-            phase(t)
-
-        return carry
-
-    lax.fori_loop(0, depth + 2, step, 0)
-    finish()
-
-
-def forward_and_gather(mesh_shape, lengths, inputs, w_qkv, b_qkv, pieces, collective_id=3):
-    depth, devices = mesh_shape["rep"], mesh_shape["rep"] * mesh_shape["fsdp"]
-    strips = strips_of([p.shape for p in pieces])
-    count = len(pieces)
-    rows, width = inputs.shape
-    seqs = lengths.shape[0]
-    pairs = width // PAIR
-    vmem = pl.BlockSpec(memory_space=pltpu.VMEM)
-    out = pl.pallas_call(
-        functools.partial(forward_kernel, depth, strips, count, pairs * 2 // (depth + 2)),
-        out_shape=[
-            jax.ShapeDtypeStruct((rows, 3 * width), BF),
-            jax.ShapeDtypeStruct((rows, width), BF),
-            jax.ShapeDtypeStruct((seqs, pairs, 2, rows // seqs), F32),
-        ]
-        + [jax.ShapeDtypeStruct((devices,) + p.shape, p.dtype) for p in pieces],
-        in_specs=[pl.BlockSpec(memory_space=pltpu.SMEM)] + [vmem] * (3 + count),
-        out_specs=[vmem] * 3 + [pl.BlockSpec(memory_space=pl.ANY)] * count,
-        scratch_shapes=gather_semaphores(strips, count, depth),
-        compiler_params=pltpu.CompilerParams(
-            collective_id=collective_id, has_side_effects=True, vmem_limit_bytes=48 * 1024 * 1024
-        ),
-        name="forward_and_gather",
-    )(lengths, inputs, w_qkv, b_qkv.reshape(1, 3 * width), *pieces)
-    return out[0], out[1], out[2], out[3:]
 
 
 def backward_kernel(depth, strips, count, heads_at_once, len_ref, x_ref, w_ref, qkv_ref, g_ref, ctx_ref, lse_ref, sum_ref, *refs):
@@ -776,16 +755,19 @@
     return jnp.sum(value.astype(F32), axis=0, keepdims=True)
 
 
-def middle_kernel(depth, strips, x_ref, ctx_ref, cot_ref, w_out_ref, w_up_ref, w_down_ref, vec_ref, b_up_ref, *refs):
-    hidden_ref, sum_ref, grad_ctx_ref, dw_out_ref, dw_up_ref, vec_out_ref, b_up_out_ref, owned_ref = refs[:8]
-    active_ref, slope_ref, low_ref, normed_ref, inverse_ref, branch_ref, terms_ref = refs[8:15]
-    begin, phase, finish = reduce_parts(depth, strips, (terms_ref,), (owned_ref,), refs[15:])
+def middle_kernel(depth, strips, x_ref, ctx_ref, cot_ref, w_out_ref, w_up_ref, w_down_ref, vec_ref, *refs):
+    hidden_ref, sum_ref, grad_ctx_ref, dw_out_ref, dw_up_ref, vec_out_ref, owned_ref = refs[:7]
+    active_ref, slope_ref, low_ref, normed_ref, inverse_ref, branch_ref, terms_ref = refs[7:14]
+    begin, phase, finish = reduce_parts(depth, strips, (terms_ref,), (owned_ref,), refs[14:])
     rows, width = x_ref.shape
     hidden = w_up_ref.shape[1]
     chunk, block = 256, 256
 
     def vector(i):
         return vec_ref[i : i + 1, :]
+
+    def up_place(j):
+        return pl.ds(8 + j // (width // block), 1), lane_block(j % (width // block), block)
 
     def put(i, value):
         vec_out_ref[i : i + 1, :] += value
@@ -807,7 +789,7 @@
 
     def up(j, carry):
         columns = lane_block(j, block)
-        inner = nn(low_ref[...], w_up_ref[:, columns]) + b_up_ref[:, columns]
+        inner = nn(low_ref[...], w_up_ref[:, columns]) + vec_ref[up_place(j)]
         half = 0.5 + 0.5 * lax.erf(inner * (2.0**-0.5))
         active_ref[:, columns] = (inner * half).astype(BF)
         slope_ref[:, columns] = (half + inner * ((2.0 * math.pi) ** -0.5) * jnp.exp(-0.5 * inner * inner)).astype(BF)
@@ -850,7 +832,7 @@
         grad_active = nt(branch_ref[...], w_down_ref[columns, :])
         grad_inner = (grad_active * slope_ref[:, columns].astype(F32)).astype(BF)
         slope_ref[:, columns] = grad_inner
-        b_up_out_ref[:, columns] = total_rows(grad_inner)
+        vec_out_ref[up_place(j)] = total_rows(grad_inner)
         dw_up_ref[:, columns] = tn(low_ref[...], grad_inner).astype(BF)
 
         @pl.when(j % stride == stride - 1)
@@ -881,7 +863,7 @@
     finish()
 
 
-def middle(mesh_shape, inputs, context, cotangent, w_out, w_up, w_down, plain, b_up, collective_id=5):
+def middle(mesh_shape, inputs, context, cotangent, w_out, w_up, w_down, vectors, collective_id=5):
     depth, devices = mesh_shape["rep"], mesh_shape["rep"] * mesh_shape["fsdp"]
     rows, width = inputs.shape
     hidden = w_up.shape[1]
@@ -897,12 +879,11 @@
             shape((rows, width), BF),
             shape((width, width), BF),
             shape((width, hidden), BF),
-            shape((8, width), F32),
-            shape((1, hidden), F32),
+            shape(vectors.shape, F32),
             shape(terms.shape[1:], F32),
         ],
-        in_specs=[vmem] * 8,
-        out_specs=[vmem] * 8,
+        in_specs=[vmem] * 7,
+        out_specs=[vmem] * 7,
         scratch_shapes=[
             pltpu.VMEM((rows, hidden), BF),
             pltpu.VMEM((rows, hidden), BF),
@@ -917,7 +898,7 @@
             collective_id=collective_id, has_side_effects=True, vmem_limit_bytes=67043328
         ),
         name="middle",
-    )(inputs, context, cotangent, w_out, w_up, w_down, plain, b_up.reshape(1, hidden))
+    )(inputs, context, cotangent, w_out, w_up, w_down, vectors)
 
 EPS = 1e-06
 AXES = ("fsdp", "rep")
@@ -951,6 +932,55 @@
 
 def reduce_native(terms):
     return [lax.psum_scatter(t.astype(F32), AXES, scatter_dimension=0, tiled=False) for t in terms]
+
+
+def local_fused(mesh_shape, hidden_in, lengths, qkv_shard, later, vectors, up_bias, cotangent):
+    seqs, length, width = hidden_in.shape
+    rows = seqs * length
+    depth = mesh_shape["rep"]
+    devices = depth * mesh_shape["fsdp"]
+    share, spread = width // devices, up_bias.shape[0] * devices // width
+    hidden = width * spread
+    me = lax.axis_index("fsdp") * depth + lax.axis_index("rep")
+    column = lax.broadcasted_iota(jnp.int32, (8, width), 1)
+    plain = jnp.where(column // share == me, jnp.tile(jnp.stack(vectors), (1, devices)), 0)
+    column = lax.broadcasted_iota(jnp.int32, (spread, width), 1) + width * lax.broadcasted_iota(jnp.int32, (spread, width), 0)
+    wide = jnp.where(column // (spread * share) == me, jnp.tile(up_bias, (spread, devices // spread)), 0)
+    slot = jnp.pad(jnp.concatenate([plain, wide]), ((0, -(8 + spread) % 16), (0, 0)))
+    inputs = hidden_in.reshape(rows, width)
+    qkv, context, log_sums, whole, w_qkv, got = forward_and_gather(mesh_shape, lengths, inputs, [slot, qkv_shard], later)
+    w_qkv = w_qkv.reshape(width, 3 * width)
+    w_out = got[0].reshape(width, width)
+    w_up = got[1].reshape(width, hidden)
+    w_down = got[2].reshape(hidden, width)
+    hidden_out, grad_first_sum, grad_context, grad_w_out, grad_w_up, sums, owned_down = middle(
+        mesh_shape, inputs, context, cotangent.reshape(rows, width), w_out, w_up, w_down, whole
+    )
+    terms = [grad_w_out.reshape(devices, share, width), grad_w_up.reshape(devices, share, hidden)]
+    grad_w_qkv, input_grad, bias_sums, owned = backward_and_reduce(
+        mesh_shape, lengths, inputs, w_qkv, qkv, grad_context, context, log_sums, grad_first_sum, terms
+    )
+    bias_sums = bias_sums.reshape(3, width)
+    plain = jnp.concatenate([bias_sums[:1], bias_sums[2:], sums[2:8]]).reshape(8, devices, share)
+    wide = sums[8 : 8 + spread].reshape(devices, spread, share)
+    vector_terms = jnp.concatenate([jnp.transpose(plain, (1, 0, 2)), wide], axis=1)
+    vector_terms = jnp.pad(vector_terms, ((0, 0), (0, -(8 + spread) % 16), (0, -share % 128)))
+    summed, owned_qkv = reduce_remote(mesh_shape, [vector_terms, grad_w_qkv.reshape(devices, share, 3 * width)])
+    vec = summed[:8, :share]
+    up = summed[8 : 8 + spread, :share].reshape(spread * share)
+    owned_qkv = [owned_qkv[:, part * width : (part + 1) * width] for part in range(3)]
+    return (
+        hidden_out.reshape(seqs, length, width),
+        input_grad.reshape(seqs, length, width),
+        *owned_qkv,
+        *owned,
+        owned_down,
+        vec[0],
+        vec[1],
+        vec[2],
+        up,
+        *(vec[i] for i in range(3, 8)),
+    )
 
 
 def local(
@@ -974,6 +1004,17 @@
     second_shift,
     cotangent,
 ):
+    if fits(mesh_shape, query_weight.shape[0]):
+        return local_fused(
+            mesh_shape,
+            hidden_in,
+            lengths,
+            jnp.concatenate([query_weight, key_weight, value_weight], axis=1),
+            [out_weight, up_weight, down_weight],
+            [query_bias, value_bias, out_bias, down_bias, first_gain, first_shift, second_gain, second_shift],
+            up_bias,
+            cotangent,
+        )
     seqs, length, width = hidden_in.shape
     rows = seqs * length
     hidden = up_weight.shape[1]
@@ -990,8 +1031,7 @@
     vector_slot = jnp.pad(vectors, ((0, -count % 16), (0, -share % 128)))
     qkv_shard = jnp.concatenate([query_weight, key_weight, value_weight], axis=1)
     later = [out_weight, up_weight, down_weight]
-    fused = fits(mesh_shape, share)
-    got = gather(mesh_shape, [vector_slot, qkv_shard])
+    got = gather_native([vector_slot, qkv_shard])
     w_qkv = got[1].reshape(width, 3 * width)
     wide = got[0].astype(F32)
     plain = jnp.transpose(wide[:, :8, :share], (1, 0, 2)).reshape(8, width)
@@ -1000,85 +1040,69 @@
 
     inputs = hidden_in.reshape(rows, width)
     b_qkv = jnp.concatenate([b_query, jnp.zeros_like(b_query), b_values])
-    if fused:
-        qkv, context, log_sums, got = forward_and_gather(mesh_shape, lengths, inputs, w_qkv, b_qkv, later)
-    else:
-        got = gather(mesh_shape, later)
-        qkv = (nn(inputs, w_qkv) + b_qkv).astype(BF)
-        context, log_sums = attention_forward(lengths, qkv, seqs, length, width)
+    got = gather_native(later)
+    qkv = (nn(inputs, w_qkv) + b_qkv).astype(BF)
+    context, log_sums = attention_forward(lengths, qkv, seqs, length, width)
     w_out = got[0].reshape(width, width)
     w_up = got[1].reshape(width, hidden)
     w_down = got[2].reshape(hidden, width)
-    if fused:
-        hidden_out, grad_first_sum, grad_context, grad_w_out, grad_w_up, vector_sums, grad_b_up, owned_down = middle(
-            mesh_shape, inputs, context, cotangent.reshape(rows, width), w_out, w_up, w_down, plain, b_up
-        )
-        hidden_out = hidden_out.reshape(seqs, length, width)
-        later = [grad_w_out.reshape(devices, share, width), grad_w_up.reshape(devices, share, hidden)]
-        grad_w_qkv, input_grad, bias_sums, owned_later = backward_and_reduce(
-            mesh_shape, lengths, inputs, w_qkv, qkv, grad_context, context, log_sums, grad_first_sum, later
-        )
-        owned_later = [owned_later[0], owned_later[1], owned_down]
-        bias_sums = bias_sums[0]
-        sums = jnp.concatenate([jnp.stack([bias_sums[:width], bias_sums[2 * width :]]), vector_sums[2:]])
-    else:
-        first_sum = inputs.astype(F32) + nn(context, w_out) + b_out
-        first, normed_one, inverse_one = norm_forward(first_sum, gain_one, shift_one)
-        first_low = first.astype(BF)
-        inner = nn(first_low, w_up) + b_up
-        half = 0.5 * (1.0 + lax.erf(inner * (2.0**-0.5)))
-        active = (inner * half).astype(BF)
-        slope = half + inner * ((2.0 * math.pi) ** -0.5) * jnp.exp(-0.5 * inner * inner)
-        slope = slope.astype(BF)
-        second_sum = first + nn(active, w_down) + b_down
-        result, normed_two, inverse_two = norm_forward(second_sum, gain_two, shift_two)
-        hidden_out = result.astype(BF).reshape(seqs, length, width)
-        grad_out = cotangent.reshape(rows, width).astype(F32)
-        grad_second, grad_gain_two, grad_shift_two = norm_backward(grad_out, normed_two, inverse_two, gain_two)
-        grad_branch = grad_second.astype(BF)
-        grad_b_down = column_sums(grad_branch)
-        grad_w_down = tn(active, grad_branch)
-        grad_active = nt(grad_branch, w_down)
-        grad_inner = (grad_active * slope.astype(F32)).astype(BF)
-        grad_b_up = column_sums(grad_inner)
-        grad_w_up = tn(first_low, grad_inner)
-        grad_first = grad_second + nt(grad_inner, w_up)
-        grad_first_sum, grad_gain_one, grad_shift_one = norm_backward(grad_first, normed_one, inverse_one, gain_one)
-        grad_attn = grad_first_sum.astype(BF)
-        grad_b_out = column_sums(grad_attn)
-        grad_w_out = tn(context, grad_attn)
-        grad_context = nt(grad_attn, w_out).astype(BF)
-        later = [
-            grad_w_out.reshape(devices, share, width),
-            grad_w_up.reshape(devices, share, hidden),
-            grad_w_down.reshape(devices, spread * share, width),
+    first_sum = inputs.astype(F32) + nn(context, w_out) + b_out
+    first, normed_one, inverse_one = norm_forward(first_sum, gain_one, shift_one)
+    first_low = first.astype(BF)
+    inner = nn(first_low, w_up) + b_up
+    half = 0.5 * (1.0 + lax.erf(inner * (2.0**-0.5)))
+    active = (inner * half).astype(BF)
+    slope = half + inner * ((2.0 * math.pi) ** -0.5) * jnp.exp(-0.5 * inner * inner)
+    slope = slope.astype(BF)
+    second_sum = first + nn(active, w_down) + b_down
+    result, normed_two, inverse_two = norm_forward(second_sum, gain_two, shift_two)
+    hidden_out = result.astype(BF).reshape(seqs, length, width)
+    grad_out = cotangent.reshape(rows, width).astype(F32)
+    grad_second, grad_gain_two, grad_shift_two = norm_backward(grad_out, normed_two, inverse_two, gain_two)
+    grad_branch = grad_second.astype(BF)
+    grad_b_down = column_sums(grad_branch)
+    grad_w_down = tn(active, grad_branch)
+    grad_active = nt(grad_branch, w_down)
+    grad_inner = (grad_active * slope.astype(F32)).astype(BF)
+    grad_b_up = column_sums(grad_inner)
+    grad_w_up = tn(first_low, grad_inner)
+    grad_first = grad_second + nt(grad_inner, w_up)
+    grad_first_sum, grad_gain_one, grad_shift_one = norm_backward(grad_first, normed_one, inverse_one, gain_one)
+    grad_attn = grad_first_sum.astype(BF)
+    grad_b_out = column_sums(grad_attn)
+    grad_w_out = tn(context, grad_attn)
+    grad_context = nt(grad_attn, w_out).astype(BF)
+    later = [
+        grad_w_out.reshape(devices, share, width),
+        grad_w_up.reshape(devices, share, hidden),
+        grad_w_down.reshape(devices, spread * share, width),
+    ]
+    grad_query, grad_keys, grad_values = attention_backward(
+        lengths, qkv, grad_context, context, log_sums, seqs, length, width
+    )
+    grad_qkv = jnp.concatenate([grad_query, grad_keys, grad_values], axis=1)
+    input_grad = (grad_first_sum + nt(grad_qkv, w_qkv)).astype(BF)
+    grad_w_qkv = tn(inputs, grad_qkv)
+    bias_sums = column_sums(grad_qkv)
+    owned_later = reduce_native(later)
+    sums = jnp.stack(
+        [
+            bias_sums[:width],
+            bias_sums[2 * width :],
+            grad_b_out,
+            grad_b_down,
+            grad_gain_one,
+            grad_shift_one,
+            grad_gain_two,
+            grad_shift_two,
         ]
-        grad_query, grad_keys, grad_values = attention_backward(
-            lengths, qkv, grad_context, context, log_sums, seqs, length, width
-        )
-        grad_qkv = jnp.concatenate([grad_query, grad_keys, grad_values], axis=1)
-        input_grad = (grad_first_sum + nt(grad_qkv, w_qkv)).astype(BF)
-        grad_w_qkv = tn(inputs, grad_qkv)
-        bias_sums = column_sums(grad_qkv)
-        owned_later = reduce_native(later)
-        sums = jnp.stack(
-            [
-                bias_sums[:width],
-                bias_sums[2 * width :],
-                grad_b_out,
-                grad_b_down,
-                grad_gain_one,
-                grad_shift_one,
-                grad_gain_two,
-                grad_shift_two,
-            ]
-        )
+    )
     input_grad = input_grad.reshape(seqs, length, width)
     vector_terms = jnp.concatenate(
         [jnp.transpose(sums.reshape(8, devices, share), (1, 0, 2)), grad_b_up.reshape(devices, spread, share)], axis=1
     )
     vector_terms = jnp.pad(vector_terms, ((0, 0), (0, -count % 16), (0, -share % 128)))
-    owned = reduce(mesh_shape, [vector_terms, grad_w_qkv.reshape(devices, share, 3 * width)])
+    owned = reduce_native([vector_terms, grad_w_qkv.reshape(devices, share, 3 * width)])
     vec = owned[0][:count, :share]
     return (
         hidden_out,

time: 280 us -> 275 us (0.982)
    pallas_call x2 -> x1, Pallas kernels: 88.5 us -> 86.3 us  [forward_and_gather(): pl.pallas_call(functools.partial(forward_kernel, depth, strips, counts),...]
    unnamed x39 -> x37, local copies, waits for them, and re-layouts: 14.6 us -> 15.2 us
where the time goes in v1:
time: 275 us; the launch traced here: 274 us
  Pallas kernels  253 us (92%)
  local copies, waits for them, and re-layouts  19.9 us (7%)
    pallas_call x1, Pallas kernels, forward_and_gather(): pl.pallas_call(functools.partial(forward_kernel, depth, strips, counts),...  86.3 us
    pallas_call x1, Pallas kernels, middle(): pl.pallas_call(functools.partial(middle_kernel, depth, strips), out_shape...  79.8 us
    pallas_call x1, Pallas kernels, backward_and_reduce(): pl.pallas_call(functools.partial(backward_kernel, depth, strips, count, p...  56 us
    pallas_call x1, Pallas kernels, reduce_remote(): pl.pallas_call(functools.partial(reduce_kernel, depth, strips, count), ou...  30.6 us
    unnamed x37, local copies, waits for them, and re-layouts  15.2 us

profile of v1, /device:TPU:0, one launch (start us, length us, event | category | flops | bytes accessed | tf_op | source)
XLA Modules:
  0.0 274.4 jit_solution(6442214461947337970)
XLA Ops:
  0.7 0.8 stack.35
  1.5 0.7 tile.21
  2.1 0.1 tile.22
  2.2 0.1 fusion.6
  2.4 0.1 tile.20
  2.5 0.8 pad_maximum_fusion.refs_1_
  3.3 0.0 copy-start
  3.4 1.4 copy-done
  4.8 0.0 copy-start.4
  4.8 0.9 copy-done.4
  5.7 0.0 copy-start.5
  5.7 0.9 copy-done.5
  6.6 0.0 copy-start.8
  6.6 0.8 copy-done.8
  7.3 0.0 copy-start.9
  7.3 0.7 copy-done.9
  8.0 86.3 %forward_and_gather.1 = (bf16[1024,2304]{1,0:T(8,128)(2,1)}, bf16[1024,768]{1,0:T(8,128)(2,1)S(1)}, f32[2,6,2,512]{3,2,1,0:T(2,128)S(1)}, f32[16,768]{1,0:T(8,12...) custom-call(s32[2]{0:T(128)S(1)} %copy-done.9, ...), custom_call_target="tpu_custom_call" | custom-call | tf_op jit(solution)/shard_map/forward_and_gather/pallas_call | solution.py:614
  94.3 0.0 copy-start.1
  94.3 1.1 copy-done.1
  95.4 0.0 copy-start.3
  95.4 1.0 copy-done.3
  96.4 0.0 copy-start.6
  96.4 0.6 copy-done.6
  97.0 0.0 copy-start.7
  97.0 0.6 copy-done.7
  97.7 79.8 %middle.1 = (bf16[1024,768]{1,0:T(8,128)(2,1)}, f32[1024,768]{1,0:T(8,128)}, bf16[1024,768]{1,0:T(8,128)(2,1)}, bf16[768,768]{1,0:T(8,128)(2,1)}, bf16[768,3072]...) custom-call(bf16[1024,768]{1,0:T(8,128)(2,1)} %bitcast.39, bf16[1024,768]{1,0:T(8,128)(2,1)} %copy-done.1, ...), custom_call_target="tpu_custom_call" | custom-call | tf_op jit(solution)/shard_map/middle/pallas_call | solution.py:874
  177.4 0.0 copy-start.15
  177.4 56.0 %backward_and_reduce.1 = (bf16[768,2304]{1,0:T(8,128)(2,1)}, bf16[1024,768]{1,0:T(8,128)(2,1)}, f32[1,2304]{1,0:T(1,128)}, f32[24,768]{1,0:T(8,128)}, f32[24,3072]{1,0:T(8,128)}) custom-call(s32[2]{0:T(128)} %len_ref.3, bf16[1024,768]{1,0:T(8,128)(2,1)} %bitcast.40, bf16[768,2304]{1,0:T(8,128)(2,1)} %bitcast.47, ...), custom_call_target="tpu_custom_call" | custom-call | tf_op jit(solution)/shard_map/backward_and_reduce/pallas_call | solution.py:720
  233.4 0.7 slice_reduce_fusion.1
  234.1 0.1 concatenate.21
  234.2 0.0 copy-done.15
  234.2 0.1 concatenate.22
  234.3 0.1 reshape.98
  234.5 0.1 concatenate.23
  234.6 0.1 copy.37
  234.6 0.1 maximum_bitcast_fusion
  234.8 0.0 copy-start.2
  234.8 2.0 copy-done.2
  236.8 0.0 copy-start.10
  236.8 30.6 %reduce_terms.1 = (f32[16,128]{1,0:T(8,128)S(1)}, f32[24,2304]{1,0:T(8,128)S(1)}) custom-call(f32[32,16,128]{2,1,0:T(8,128)S(1)} %select_maximum_fusion.refs_0_, bf16[32,24,2304]{2,1,0:T(8,128)(2,1)S(1)} %bitcast.42), custom_call_target="tpu_custom_call" | custom-call | tf_op jit(solution)/shard_map/reduce_terms/pallas_call | solution.py:651
  267.4 0.7 fusion.10
  268.1 0.5 slice_bitcast_fusion
  268.6 0.6 reshape.100
  269.2 0.0 copy-done.10
  269.2 0.0 copy-start.11
  269.2 1.1 copy.43
  270.4 0.8 copy-done.11
  271.2 0.0 copy-start.14
  271.2 0.0 copy-start.13
  271.2 0.0 copy-start.12
  271.2 1.1 copy.44
  272.4 0.0 copy-done.14
  272.4 0.6 copy.45
  273.0 0.0 copy-done.13
  273.0 0.7 copy.46
  273.7 0.0 copy-done.12
  273.7 0.7 copy.47
  (10 shorter events, 0.1 us)
Async XLA Ops:
  3.3 1.4 copy-start
  4.8 0.9 copy-start.4
  5.7 0.9 copy-start.5
  6.6 0.8 copy-start.8
  7.3 0.7 copy-start.9
  94.3 1.1 copy-start.1
  95.4 1.0 copy-start.3
  96.4 0.6 copy-start.6
  97.0 0.6 copy-start.7
  177.4 56.8 %copy-start.15 = (f32[16,768]{1,0:T(8,128)S(1)}, f32[16,768]{1,0:T(8,128)}, u32[]{:S(2)}) copy-start(f32[16,768]{1,0:T(8,128)} %get-tuple-element.54) | copy-start | bytes 147460
  234.8 2.0 copy-start.2
  236.8 32.5 %copy-start.10 = (bf16[1024,768]{1,0:T(8,128)(2,1)S(1)}, bf16[1024,768]{1,0:T(8,128)(2,1)}, u32[]{:S(2)}) copy-start(bf16[1024,768]{1,0:T(8,128)(2,1)} %get-tuple-element.44) | copy-start | bytes 4718596
  269.2 2.0 copy-start.11
  271.2 1.2 copy-start.14
  271.2 1.8 copy-start.13
  271.2 2.5 copy-start.12
